TPU v7x, 32 devices: a whole 2x2x4 slice. The times are simulated.
32 devices in a mesh: py: 2 (over x), px: 4 (over z), pz: 4 (over y, core).
Axes of the slice: x: 2, y: 2, z: 4, core: 2. Of those that a mesh axis runs over, the one named last changes fastest.
Arguments:
- field_now: float32 [16, 64, 256, 128], P('py', 'px', 'pz'), may hold values from 0.2 to 1.8
- earlier: float32 [16, 64, 256, 128], P('py', 'px', 'pz'), may hold values from 0.2 to 1.8
- speed_square: float32 [16, 64, 256, 128], P('py', 'px', 'pz'), may hold values from 0.05 to 0.3
Outputs:
- column_sum: float32 [16, 64, 256, 128], P('py', 'px', 'pz')
- field_now_end: float32 [16, 64, 256, 128], P('py', 'px', 'pz')
All inputs are finite; a program needn't handle non-finite values.
Results may differ from a plain program's by a relative error of at most 0.00002.
Values sent between devices are 32-bit elements; how exact they have to be, the bound alone decides.
A program may use at most 128 MiB of HBM per device.

v0:
```python
import functools

import jax
import jax.numpy as jnp
from jax import lax
from jax.experimental import pallas as pl
from jax.experimental.pallas import tpu as pltpu
from jax.sharding import PartitionSpec as P

STEPS = 4
CHUNKS = 4
MESH = pl.DeviceIdType.MESH


def march_kernel(
    peers, chunks, field, before, speed, end, under,
    u, cs, total, below, ysend, yrecv,
    load_sem, x_send, x_recv, z_send, z_recv, y_send, y_recv, t_send, t_recv, word,
):
    J, I, K, L = field.shape
    ny, nx, nz = peers
    width = I // chunks
    my, mx, mz = (lax.axis_index(a) for a in ("py", "px", "pz"))
    y_side = ({"py": lax.rem(my + 1, ny)}, {"py": lax.rem(my + ny - 1, ny)})
    x_side = ({"px": lax.rem(mx + 1, nx)}, {"px": lax.rem(mx + nx - 1, nx)})
    z_side = ({"pz": lax.rem(mz + 1, nz)}, {"pz": lax.rem(mz + nz - 1, nz)})
    parts = ((1, J - 2), (0, 1), (J - 1, 1))

    loads = [
        pltpu.make_async_copy(
            field.at[pl.ds(start, size)], u.at[0, pl.ds(start + 1, size), pl.ds(1, I)], load_sem.at[part]
        )
        for part, (start, size) in reversed(tuple(enumerate(parts)))
    ] + [
        pltpu.make_async_copy(before, u.at[1, pl.ds(1, J), pl.ds(1, I)], load_sem.at[3]),
        pltpu.make_async_copy(speed, cs, load_sem.at[4]),
    ]
    barrier = pltpu.get_barrier_semaphore()
    above, under_me = mx < nx - 1, mx > 0

    def greet(to):
        pl.semaphore_signal(barrier, inc=1, device_id=to, device_id_type=MESH)

    for d in range(1, ny):
        greet({"py": lax.rem(my + d, ny)})
    for side in z_side:
        greet(side)

    @pl.when(above)
    def _():
        greet(x_side[0])

    @pl.when(under_me)
    def _():
        greet(x_side[1])

    for load in loads[:2]:
        load.start()
    pl.semaphore_wait(barrier, ny - 1 + 2 + jnp.where(above, 1, 0) + jnp.where(under_me, 1, 0))

    def hand_on():
        for way, (comes, goes) in enumerate(((under_me, above), (above, under_me))):
            @pl.when(comes)
            def _(way=way):
                pl.semaphore_wait(word.at[way], 1)

            @pl.when(goes)
            def _(way=way):
                pl.semaphore_signal(word.at[way], inc=1, device_id=x_side[way], device_id_type=MESH)

    def remote(src, dst, send, recv, to):
        return pltpu.make_async_remote_copy(
            src_ref=src, dst_ref=dst, send_sem=send, recv_sem=recv, device_id=to, device_id_type=MESH
        )

    def j_copy(t, side, c):
        row, rim = ((J - 1, 0), (0, J + 1))[side]
        there = pl.ds(1 + c * width, width)
        return remote(u.at[t % 2, row + 1, there], u.at[t % 2, rim, there], x_send.at[t, side, c], x_recv.at[t, side, c], y_side[side])

    def i_copy(t, side, part):
        plane, rim = ((I - 1, 0), (0, I + 1))[side]
        start, size = parts[part]
        rows = pl.ds(start + 1, size)
        src = field.at[pl.ds(start, size), plane] if t == 0 else u.at[t % 2, rows, plane + 1]
        return remote(src, u.at[t % 2, rows, rim], z_send.at[t, side, part], z_recv.at[t, side, part], x_side[side])

    def k_copy(t, side, part):
        start, size = parts[part]
        rows = pl.ds(start, size)
        return remote(
            ysend.at[t, side, rows], yrecv.at[t, side, rows],
            y_send.at[t, side, part], y_recv.at[t, side, part], z_side[side],
        )

    def pack(t, j, i, value):
        ysend[t, 0, j, pl.ds(i, 1), :] = value[K - 1:K]
        ysend[t, 1, j, pl.ds(i, 1), :] = value[0:1]

    for side in (0, 1):
        loads[side].wait()
    for c in range(chunks):
        for side in (0, 1):
            j_copy(0, side, c).start()
    for load in loads[2:]:
        load.start()
    hand_on()
    for part in range(3):
        for side in (0, 1):
            i_copy(0, side, part).start()

    loads[2].wait()

    def pack_row(j, carry):
        for i in range(I):
            ysend[0, 0, j, i:i + 1, :] = u[0, j + 1, i + 1, K - 1:K, :]
            ysend[0, 1, j, i:i + 1, :] = u[0, j + 1, i + 1, 0:1, :]
        return carry

    lax.fori_loop(0, J, pack_row, 0)
    for part in range(3):
        for side in (0, 1):
            k_copy(0, side, part).start()
    loads[3].wait()
    loads[4].wait()

    k_index = lax.broadcasted_iota(jnp.int32, (K, L), 0)

    def column(t, j, i):
        now, other = t % 2, (t + 1) % 2
        middle = u[now, j + 1, i + 1]
        low = jnp.where(k_index == 0, yrecv[t, 0, j, pl.ds(i, 1), :], pltpu.roll(middle, 1, 0))
        high = jnp.where(k_index == K - 1, yrecv[t, 1, j, pl.ds(i, 1), :], pltpu.roll(middle, K - 1, 0))
        spread = (
            u[now, j, i + 1] + u[now, j + 2, i + 1] + u[now, j + 1, i] + u[now, j + 1, i + 2]
            + low + high - 6.0 * middle
        )
        later = 2.0 * middle - u[other, j + 1, i + 1] + cs[j, i] * spread
        if t + 1 < STEPS:
            u[other, j + 1, i + 1] = later
            pack(t + 1, j, i, later)
        else:
            end[j, i] = later

    def total_copy(d, c):
        here = pl.ds(c * width, width)
        return remote(
            total.at[here], below.at[d - 1, here], t_send.at[d - 1, c], t_recv.at[d - 1, c],
            {"py": lax.rem(my + d, ny)},
        )

    for t in range(STEPS):
        last = t + 1 == STEPS
        for side in (0, 1):
            i_copy(t, side, 0).wait_recv()
            k_copy(t, side, 0).wait_recv()
            if t > 0:
                i_copy(t - 1, side, 0).wait_send()

        def inner(q, carry, t=t):
            j = 1 + q // (I // 2)
            i = lax.rem(q, I // 2) * 2
            column(t, j, i)
            column(t, j, i + 1)
            return carry

        lax.fori_loop(0, (J - 2) * (I // 2), inner, 0)
        if not last:
            for side in (0, 1):
                i_copy(t + 1, side, 0).start()
                k_copy(t + 1, side, 0).start()

        for side in (0, 1):
            for part in (1, 2):
                i_copy(t, side, part).wait_recv()
                k_copy(t, side, part).wait_recv()
                if t > 0:
                    i_copy(t - 1, side, part).wait_send()
        for c in range(chunks):
            for side in (0, 1):
                j_copy(t, side, c).wait_recv()
                if t > 0:
                    j_copy(t - 1, side, c).wait_send()

            def outer(q, carry, t=t, c=c):
                i = c * width + q
                column(t, 0, i)
                column(t, J - 1, i)
                return carry

            lax.fori_loop(0, width, outer, 0)
            if not last:
                for side in (0, 1):
                    j_copy(t + 1, side, c).start()
            else:
                def add_up(q, carry, c=c):
                    i = c * width + q
                    value = end[0, i]
                    for j in range(1, J):
                        value = value + end[j, i]
                    total[i] = value
                    return carry

                lax.fori_loop(0, width, add_up, 0)
                for d in range(1, ny):
                    @pl.when(my + d < ny)
                    def _(d=d, c=c):
                        total_copy(d, c).start()
        if not last:
            for part in (1, 2):
                for side in (0, 1):
                    i_copy(t + 1, side, part).start()
                    k_copy(t + 1, side, part).start()

    for c in range(chunks):
        here = pl.ds(c * width, width)
        under[here] = jnp.zeros((width, K, L), jnp.float32)
        for d in range(1, ny):
            @pl.when(my >= d)
            def _(d=d, c=c, here=here):
                total_copy(d, c).wait_recv()
                under[here] = under[here] + below[d - 1, here]

    for side in (0, 1):
        for c in range(chunks):
            j_copy(STEPS - 1, side, c).wait_send()
        for part in range(3):
            i_copy(STEPS - 1, side, part).wait_send()
            for t in range(STEPS):
                k_copy(t, side, part).wait_send()
    for c in range(chunks):
        for d in range(1, ny):
            @pl.when(my + d < ny)
            def _(d=d, c=c):
                total_copy(d, c).wait_send()


def sums_kernel(scale, chunks, end, under, sums_out, field_out, csum, sum_sem, out_sem):
    J, I = end.shape[:2]
    width = I // chunks

    def out_copy(c):
        here = pl.ds(c * width, width)
        return pltpu.make_async_copy(end.at[:, here], field_out.at[:, here], out_sem.at[c])

    def sum_copy(c):
        here = pl.ds(c * width, width)
        return pltpu.make_async_copy(csum.at[:, here], sums_out.at[:, here], sum_sem.at[c])

    for c in range(chunks):
        out_copy(c).start()
    for c in range(chunks):
        def running(q, carry, c=c):
            i = c * width + q
            value = under[i]
            for j in range(J):
                value = value + end[j, i]
                csum[j, i] = value * scale
            return carry

        lax.fori_loop(0, width, running, 0)
        sum_copy(c).start()
    for c in range(chunks):
        out_copy(c).wait()
        sum_copy(c).wait()


def local(peers, field_now, earlier, speed_square):
    J, I, K, L = field_now.shape
    chunks = CHUNKS if I % CHUNKS == 0 else 1
    ny = peers[0]
    f32 = jnp.float32
    dma = pltpu.SemaphoreType.DMA
    anywhere = pl.BlockSpec(memory_space=pltpu.MemorySpace.HBM)
    shape = jax.ShapeDtypeStruct(field_now.shape, f32)
    slots = max(ny - 1, 1)
    resident = pl.BlockSpec(memory_space=pltpu.VMEM)
    end, under = pl.pallas_call(
        functools.partial(march_kernel, peers, chunks),
        out_shape=(pltpu.VMEM((J, I, K, L), f32), pltpu.VMEM((I, K, L), f32)),
        in_specs=[anywhere] * 3,
        out_specs=(resident, resident),
        scratch_shapes=[
            pltpu.VMEM((2, J + 2, I + 2, K, L), f32),
            pltpu.VMEM((J, I, K, L), f32),
            pltpu.VMEM((I, K, L), f32),
            pltpu.VMEM((slots, I, K, L), f32),
            pltpu.VMEM((STEPS, 2, J, I, L), f32),
            pltpu.VMEM((STEPS, 2, J, I, L), f32),
            dma((5,)),
            dma((STEPS, 2, chunks)),
            dma((STEPS, 2, chunks)),
            dma((STEPS, 2, 3)),
            dma((STEPS, 2, 3)),
            dma((STEPS, 2, 3)),
            dma((STEPS, 2, 3)),
            dma((slots, chunks)),
            dma((slots, chunks)),
            pltpu.SemaphoreType.REGULAR((2,)),
        ],
        compiler_params=pltpu.CompilerParams(
            collective_id=0, has_side_effects=True, vmem_limit_bytes=55 * 1024 * 1024
        ),
        name="march",
    )(field_now, earlier, speed_square)
    return pl.pallas_call(
        functools.partial(sums_kernel, 1.0 / (J * ny), chunks),
        out_shape=(shape, shape),
        in_specs=[resident] * 2,
        out_specs=(anywhere, anywhere),
        scratch_shapes=[pltpu.VMEM((J, I, K, L), f32), dma((chunks,)), dma((chunks,))],
        compiler_params=pltpu.CompilerParams(vmem_limit_bytes=16 * 1024 * 1024),
        name="sums",
    )(end, under)


def solution(mesh):
    placed = P("py", "px", "pz", None)
    peers = tuple(mesh.shape[a] for a in ("py", "px", "pz"))
    return jax.shard_map(
        functools.partial(local, peers),
        mesh=mesh,
        in_specs=(placed,) * 3,
        out_specs=(placed,) * 2,
        check_vma=False,
    )
```

profile of v0, /device:TPU:0, one launch (start us, length us, event | category | flops | bytes accessed | tf_op | source)
XLA Modules:
  0.0 110.3 jit_solution(14398247628325664768)
XLA Ops:
  0.6 106.2 %march.1 = (f32[8,16,64,128]{3,2,1,0:T(8,128)S(1)}, f32[16,64,128]{2,1,0:T(8,128)S(1)}) custom-call(f32[8,16,64,128]{3,2,1,0:T(8,128)} %field.1, f32[8,16,64,128]{3,2,1,0:T(8,128)} %before.1, f32[8,16,64,128]{3,2,1,0:T(8,128)} %speed.1), custom_call_target="tpu_custom_call" | custom-call | tf_op jit(solution)/shard_map/march/pallas_call | solution.py:278
  106.9 3.4 %sums.1 = (f32[8,16,64,128]{3,2,1,0:T(8,128)}, f32[8,16,64,128]{3,2,1,0:T(8,128)}) custom-call(f32[8,16,64,128]{3,2,1,0:T(8,128)S(1)} %get-tuple-element.4.end, f32[16,64,128]{2,1,0:T(8,128)S(1)} %get-tuple-element.5.under), custom_call_target="tpu_custom_call" | custom-call | tf_op jit(solution)/shard_map/sums/pallas_call | solution.py:306
where the time goes:
time: 110 us
  Pallas kernels  110 us (100%)
    pallas_call x1, Pallas kernels, local(): pl.pallas_call(functools.partial(march_kernel, peers, chunks), out_shape=...  106 us
    pallas_call x1, Pallas kernels, local(): pl.pallas_call(functools.partial(sums_kernel, 1.0 / (J * ny), chunks), ou...  3.37 us

commit v1 on v0

--- a/solution.py
+++ b/solution.py
@@ -8,14 +8,15 @@
 from jax.sharding import PartitionSpec as P
 
 STEPS = 4
-CHUNKS = 4
+CHUNKS = 2
+OUT_CHUNKS = 4
 MESH = pl.DeviceIdType.MESH
 
 
 def march_kernel(
     peers, chunks, field, before, speed, end, under,
     u, cs, total, below, ysend, yrecv,
-    load_sem, x_send, x_recv, z_send, z_recv, y_send, y_recv, t_send, t_recv, word,
+    load_sem, x_send, x_recv, z_send, z_recv, y_send, y_recv, t_send, t_recv, word, ready,
 ):
     J, I, K, L = field.shape
     ny, nx, nz = peers
@@ -37,26 +38,39 @@
     ]
     barrier = pltpu.get_barrier_semaphore()
     above, under_me = mx < nx - 1, mx > 0
+    pairs = [(mx < nx - 1, x_side[0], mx > 0, x_side[1])]
+    if nz > 1:
+        pairs.append((mz < nz - 1, z_side[0], mz > 0, z_side[1]))
+    if nz > 2:
+        pairs.append((mz == 0, z_side[1], mz == nz - 1, z_side[0]))
 
     def greet(to):
         pl.semaphore_signal(barrier, inc=1, device_id=to, device_id_type=MESH)
 
     for d in range(1, ny):
         greet({"py": lax.rem(my + d, ny)})
-    for side in z_side:
-        greet(side)
-
-    @pl.when(above)
-    def _():
-        greet(x_side[0])
-
-    @pl.when(under_me)
-    def _():
-        greet(x_side[1])
+    expected = ny - 1
+    for has_upper, upper, has_lower, _ in pairs:
+        @pl.when(has_upper)
+        def _(upper=upper):
+            greet(upper)
+
+        expected = expected + jnp.where(has_lower, 1, 0)
 
     for load in loads[:2]:
         load.start()
-    pl.semaphore_wait(barrier, ny - 1 + 2 + jnp.where(above, 1, 0) + jnp.where(under_me, 1, 0))
+    pl.semaphore_wait(barrier, expected)
+
+    def meet():
+        for n, (_, _, has_lower, lower) in enumerate(pairs):
+            @pl.when(has_lower)
+            def _(n=n, lower=lower):
+                pl.semaphore_signal(ready.at[n], inc=1, device_id=lower, device_id_type=MESH)
+
+        for n, (has_upper, _, _, _) in enumerate(pairs):
+            @pl.when(has_upper)
+            def _(n=n):
+                pl.semaphore_wait(ready.at[n], 1)
 
     def hand_on():
         for way, (comes, goes) in enumerate(((under_me, above), (above, under_me))):
@@ -73,9 +87,17 @@
             src_ref=src, dst_ref=dst, send_sem=send, recv_sem=recv, device_id=to, device_id_type=MESH
         )
 
+    def order(t):
+        return (0, 1) if t % 2 == 0 else (1, 0)
+
+    def cuts(t, side):
+        n = chunks if t + 1 == STEPS and side == order(t)[1] else 1
+        return range(n), I // n
+
     def j_copy(t, side, c):
         row, rim = ((J - 1, 0), (0, J + 1))[side]
-        there = pl.ds(1 + c * width, width)
+        size = cuts(t, side)[1]
+        there = pl.ds(1 + c * size, size)
         return remote(u.at[t % 2, row + 1, there], u.at[t % 2, rim, there], x_send.at[t, side, c], x_recv.at[t, side, c], y_side[side])
 
     def i_copy(t, side, part):
@@ -97,13 +119,13 @@
         ysend[t, 0, j, pl.ds(i, 1), :] = value[K - 1:K]
         ysend[t, 1, j, pl.ds(i, 1), :] = value[0:1]
 
-    for side in (0, 1):
-        loads[side].wait()
-    for c in range(chunks):
-        for side in (0, 1):
-            j_copy(0, side, c).start()
+    loads[0].wait()
+    j_copy(0, 0, 0).start()
+    loads[1].wait()
+    j_copy(0, 1, 0).start()
     for load in loads[2:]:
         load.start()
+    meet()
     hand_on()
     for part in range(3):
         for side in (0, 1):
@@ -170,47 +192,47 @@
                 i_copy(t + 1, side, 0).start()
                 k_copy(t + 1, side, 0).start()
 
-        for side in (0, 1):
-            for part in (1, 2):
+        for s in order(t):
+            row, part = ((0, 1), (J - 1, 2))[s]
+            for side in (0, 1):
                 i_copy(t, side, part).wait_recv()
                 k_copy(t, side, part).wait_recv()
                 if t > 0:
                     i_copy(t - 1, side, part).wait_send()
-        for c in range(chunks):
-            for side in (0, 1):
-                j_copy(t, side, c).wait_recv()
-                if t > 0:
-                    j_copy(t - 1, side, c).wait_send()
-
-            def outer(q, carry, t=t, c=c):
-                i = c * width + q
-                column(t, 0, i)
-                column(t, J - 1, i)
+            if t > 0:
+                j_copy(t - 1, 1 - s, 0).wait_send()
+
+            def outer(i, carry, t=t, row=row):
+                column(t, row, i)
                 return carry
 
-            lax.fori_loop(0, width, outer, 0)
             if not last:
-                for side in (0, 1):
-                    j_copy(t + 1, side, c).start()
-            else:
-                def add_up(q, carry, c=c):
-                    i = c * width + q
-                    value = end[0, i]
-                    for j in range(1, J):
-                        value = value + end[j, i]
-                    total[i] = value
-                    return carry
-
-                lax.fori_loop(0, width, add_up, 0)
-                for d in range(1, ny):
-                    @pl.when(my + d < ny)
-                    def _(d=d, c=c):
-                        total_copy(d, c).start()
-        if not last:
-            for part in (1, 2):
+                j_copy(t, s, 0).wait_recv()
+                pieces, size = cuts(t + 1, 1 - s)
+                for c in pieces:
+                    lax.fori_loop(c * size, (c + 1) * size, outer, 0)
+                    j_copy(t + 1, 1 - s, c).start()
                 for side in (0, 1):
                     i_copy(t + 1, side, part).start()
                     k_copy(t + 1, side, part).start()
+            else:
+                pieces, size = cuts(t, s)
+                for c in pieces:
+                    j_copy(t, s, c).wait_recv()
+                    lax.fori_loop(c * size, (c + 1) * size, outer, 0)
+                    if s == order(t)[1]:
+                        def add_up(i, carry):
+                            value = end[0, i]
+                            for j in range(1, J):
+                                value = value + end[j, i]
+                            total[i] = value
+                            return carry
+
+                        lax.fori_loop(c * size, (c + 1) * size, add_up, 0)
+                        for d in range(1, ny):
+                            @pl.when(my + d < ny)
+                            def _(d=d, c=c):
+                                total_copy(d, c).start()
 
     for c in range(chunks):
         here = pl.ds(c * width, width)
@@ -222,7 +244,7 @@
                 under[here] = under[here] + below[d - 1, here]
 
     for side in (0, 1):
-        for c in range(chunks):
+        for c in cuts(STEPS - 1, side)[0]:
             j_copy(STEPS - 1, side, c).wait_send()
         for part in range(3):
             i_copy(STEPS - 1, side, part).wait_send()
@@ -268,6 +290,7 @@
 def local(peers, field_now, earlier, speed_square):
     J, I, K, L = field_now.shape
     chunks = CHUNKS if I % CHUNKS == 0 else 1
+    out_chunks = OUT_CHUNKS if I % OUT_CHUNKS == 0 else 1
     ny = peers[0]
     f32 = jnp.float32
     dma = pltpu.SemaphoreType.DMA
@@ -297,6 +320,7 @@
             dma((slots, chunks)),
             dma((slots, chunks)),
             pltpu.SemaphoreType.REGULAR((2,)),
+            pltpu.SemaphoreType.REGULAR((3,)),
         ],
         compiler_params=pltpu.CompilerParams(
             collective_id=0, has_side_effects=True, vmem_limit_bytes=55 * 1024 * 1024
@@ -304,11 +328,11 @@
         name="march",
     )(field_now, earlier, speed_square)
     return pl.pallas_call(
-        functools.partial(sums_kernel, 1.0 / (J * ny), chunks),
+        functools.partial(sums_kernel, 1.0 / (J * ny), out_chunks),
         out_shape=(shape, shape),
         in_specs=[resident] * 2,
         out_specs=(anywhere, anywhere),
-        scratch_shapes=[pltpu.VMEM((J, I, K, L), f32), dma((chunks,)), dma((chunks,))],
+        scratch_shapes=[pltpu.VMEM((J, I, K, L), f32), dma((out_chunks,)), dma((out_chunks,))],
         compiler_params=pltpu.CompilerParams(vmem_limit_bytes=16 * 1024 * 1024),
         name="sums",
     )(end, under)

time: 110 us -> 110 us (level)
  no operation moved by 1% of the time
where the time goes in v1:
time: 110 us; the launch traced here: 109 us
  Pallas kernels  109 us (99%)
    pallas_call x1, Pallas kernels, local(): pl.pallas_call(functools.partial(march_kernel, peers, chunks), out_shape=...  105 us
    pallas_call x1, Pallas kernels, local(): pl.pallas_call(functools.partial(sums_kernel, 1.0 / (J * ny), out_chunks)...  3.37 us

profile of v1, /device:TPU:0, one launch (start us, length us, event | category | flops | bytes accessed | tf_op | source)
XLA Modules:
  0.0 109.4 jit_solution(3553097624905698001)
XLA Ops:
  0.6 105.3 %march.1 = (f32[8,16,64,128]{3,2,1,0:T(8,128)S(1)}, f32[16,64,128]{2,1,0:T(8,128)S(1)}) custom-call(f32[8,16,64,128]{3,2,1,0:T(8,128)} %field.1, f32[8,16,64,128]{3,2,1,0:T(8,128)} %before.1, f32[8,16,64,128]{3,2,1,0:T(8,128)} %speed.1), custom_call_target="tpu_custom_call" | custom-call | tf_op jit(solution)/shard_map/march/pallas_call | solution.py:301
  106.0 3.4 %sums.1 = (f32[8,16,64,128]{3,2,1,0:T(8,128)}, f32[8,16,64,128]{3,2,1,0:T(8,128)}) custom-call(f32[8,16,64,128]{3,2,1,0:T(8,128)S(1)} %get-tuple-element.4.end, f32[16,64,128]{2,1,0:T(8,128)S(1)} %get-tuple-element.5.under), custom_call_target="tpu_custom_call" | custom-call | tf_op jit(solution)/shard_map/sums/pallas_call | solution.py:330

commit v2 on v1

--- a/solution.py
+++ b/solution.py
@@ -8,24 +8,25 @@
 from jax.sharding import PartitionSpec as P
 
 STEPS = 4
-CHUNKS = 2
 OUT_CHUNKS = 4
+FIRST = (1, 2)
 MESH = pl.DeviceIdType.MESH
 
 
 def march_kernel(
-    peers, chunks, field, before, speed, end, under,
-    u, cs, total, below, ysend, yrecv,
+    peers, split, field, before, speed, end, under, total,
+    u, cs, below, ysend, yrecv,
     load_sem, x_send, x_recv, z_send, z_recv, y_send, y_recv, t_send, t_recv, word, ready,
 ):
     J, I, K, L = field.shape
     ny, nx, nz = peers
-    width = I // chunks
     my, mx, mz = (lax.axis_index(a) for a in ("py", "px", "pz"))
     y_side = ({"py": lax.rem(my + 1, ny)}, {"py": lax.rem(my + ny - 1, ny)})
     x_side = ({"px": lax.rem(mx + 1, nx)}, {"px": lax.rem(mx + nx - 1, nx)})
     z_side = ({"pz": lax.rem(mz + 1, nz)}, {"pz": lax.rem(mz + nz - 1, nz)})
     parts = ((1, J - 2), (0, 1), (J - 1, 1))
+    halves = ((0, split), (split, I - split))
+    second_core = lax.rem(mz, 2) == 1
 
     loads = [
         pltpu.make_async_copy(
@@ -91,13 +92,12 @@
         return (0, 1) if t % 2 == 0 else (1, 0)
 
     def cuts(t, side):
-        n = chunks if t + 1 == STEPS and side == order(t)[1] else 1
-        return range(n), I // n
+        return halves if t + 1 == STEPS and side == order(t)[1] else ((0, I),)
 
     def j_copy(t, side, c):
         row, rim = ((J - 1, 0), (0, J + 1))[side]
-        size = cuts(t, side)[1]
-        there = pl.ds(1 + c * size, size)
+        start, size = cuts(t, side)[c]
+        there = pl.ds(1 + start, size)
         return remote(u.at[t % 2, row + 1, there], u.at[t % 2, rim, there], x_send.at[t, side, c], x_recv.at[t, side, c], y_side[side])
 
     def i_copy(t, side, part):
@@ -164,12 +164,17 @@
         else:
             end[j, i] = later
 
-    def total_copy(d, c):
-        here = pl.ds(c * width, width)
+    def total_copy(d, first):
+        here = pl.ds(0, split if first else I)
         return remote(
-            total.at[here], below.at[d - 1, here], t_send.at[d - 1, c], t_recv.at[d - 1, c],
-            {"py": lax.rem(my + d, ny)},
-        )
+            total.at[here], below.at[d - 1, here], t_send.at[d - 1], t_recv.at[d - 1], {"py": lax.rem(my + d, ny)}
+        )
+
+    def for_totals(mine, first, act):
+        for d in range(1, ny):
+            @pl.when(jnp.logical_and(second_core if first else jnp.logical_not(second_core), my + d < ny if mine else my >= d))
+            def _(d=d):
+                act(total_copy(d, first), d)
 
     for t in range(STEPS):
         last = t + 1 == STEPS
@@ -202,140 +207,223 @@
             if t > 0:
                 j_copy(t - 1, 1 - s, 0).wait_send()
 
-            def outer(i, carry, t=t, row=row):
+            def outer(i, carry, t=t, row=row, s=s):
                 column(t, row, i)
+                if t + 1 == STEPS and s == order(t)[1]:
+                    total[i] = total[i] + end[row, i]
                 return carry
+
+            if last and s == order(t)[1]:
+                def add_up(i, carry, row=row):
+                    value, *others = (end[j, i] for j in range(J) if j != row)
+                    for other in others:
+                        value = value + other
+                    total[i] = value
+                    return carry
+
+                lax.fori_loop(0, I, add_up, 0)
 
             if not last:
                 j_copy(t, s, 0).wait_recv()
-                pieces, size = cuts(t + 1, 1 - s)
-                for c in pieces:
-                    lax.fori_loop(c * size, (c + 1) * size, outer, 0)
+                for c, (start, size) in enumerate(cuts(t + 1, 1 - s)):
+                    lax.fori_loop(start, start + size, outer, 0)
                     j_copy(t + 1, 1 - s, c).start()
                 for side in (0, 1):
                     i_copy(t + 1, side, part).start()
                     k_copy(t + 1, side, part).start()
             else:
-                pieces, size = cuts(t, s)
-                for c in pieces:
+                for c, (start, size) in enumerate(cuts(t, s)):
                     j_copy(t, s, c).wait_recv()
-                    lax.fori_loop(c * size, (c + 1) * size, outer, 0)
+                    lax.fori_loop(start, start + size, outer, 0)
                     if s == order(t)[1]:
-                        def add_up(i, carry):
-                            value = end[0, i]
-                            for j in range(1, J):
-                                value = value + end[j, i]
-                            total[i] = value
-                            return carry
-
-                        lax.fori_loop(c * size, (c + 1) * size, add_up, 0)
-                        for d in range(1, ny):
-                            @pl.when(my + d < ny)
-                            def _(d=d, c=c):
-                                total_copy(d, c).start()
-
-    for c in range(chunks):
-        here = pl.ds(c * width, width)
-        under[here] = jnp.zeros((width, K, L), jnp.float32)
-        for d in range(1, ny):
-            @pl.when(my >= d)
-            def _(d=d, c=c, here=here):
-                total_copy(d, c).wait_recv()
-                under[here] = under[here] + below[d - 1, here]
+                        for_totals(True, c == 0, lambda copy, d: copy.start())
+
+    under[...] = jnp.zeros((I, K, L), jnp.float32)
+    for first in (True, False):
+        def take(copy, d, size=split if first else I):
+            copy.wait_recv()
+            under[:size] = under[:size] + below[d - 1, :size]
+
+        for_totals(False, first, take)
 
     for side in (0, 1):
-        for c in cuts(STEPS - 1, side)[0]:
+        for c in range(len(cuts(STEPS - 1, side))):
             j_copy(STEPS - 1, side, c).wait_send()
         for part in range(3):
             i_copy(STEPS - 1, side, part).wait_send()
             for t in range(STEPS):
                 k_copy(t, side, part).wait_send()
-    for c in range(chunks):
+    for first in (True, False):
+        for_totals(True, first, lambda copy, d: copy.wait_send())
+
+
+def rest_kernel(ny, split, total, under, _, under_rest, below, send, recv):
+    size = total.shape[0] - split
+    my = lax.axis_index("py")
+    there = pl.ds(split, size)
+    second_core = lax.rem(lax.axis_index("pz"), 2) == 1
+
+    def copy(d):
+        return pltpu.make_async_remote_copy(
+            src_ref=total.at[there], dst_ref=below.at[d - 1], send_sem=send.at[d - 1], recv_sem=recv.at[d - 1],
+            device_id={"py": lax.rem(my + d, ny)}, device_id_type=MESH,
+        )
+
+    under_rest[...] = under[split:]
+
+    @pl.when(second_core)
+    def _():
+        barrier = pltpu.get_barrier_semaphore()
+        for d in range(1, ny):
+            @pl.when(my >= d)
+            def _(d=d):
+                pl.semaphore_signal(barrier, inc=1, device_id={"py": lax.rem(my + ny - d, ny)}, device_id_type=MESH)
+
+        @pl.when(my < ny - 1)
+        def _():
+            pl.semaphore_wait(barrier, ny - 1 - my)
+
         for d in range(1, ny):
             @pl.when(my + d < ny)
-            def _(d=d, c=c):
-                total_copy(d, c).wait_send()
-
-
-def sums_kernel(scale, chunks, end, under, sums_out, field_out, csum, sum_sem, out_sem):
-    J, I = end.shape[:2]
-    width = I // chunks
-
-    def out_copy(c):
-        here = pl.ds(c * width, width)
-        return pltpu.make_async_copy(end.at[:, here], field_out.at[:, here], out_sem.at[c])
+            def _(d=d):
+                copy(d).start()
+
+        for d in range(1, ny):
+            @pl.when(my >= d)
+            def _(d=d):
+                copy(d).wait_recv()
+                under_rest[...] = under_rest[...] + below[d - 1]
+
+        for d in range(1, ny):
+            @pl.when(my + d < ny)
+            def _(d=d):
+                copy(d).wait_send()
+
+
+def columns_out(scale, chunks, start, size, end, under, sums_out, csum, sem):
+    J = end.shape[0]
+    width = size // chunks
 
     def sum_copy(c):
         here = pl.ds(c * width, width)
-        return pltpu.make_async_copy(csum.at[:, here], sums_out.at[:, here], sum_sem.at[c])
+        return pltpu.make_async_copy(csum.at[:, here], sums_out.at[:, pl.ds(start + c * width, width)], sem.at[c])
 
     for c in range(chunks):
-        out_copy(c).start()
-    for c in range(chunks):
-        def running(q, carry, c=c):
-            i = c * width + q
+        def running(i, carry):
             value = under[i]
             for j in range(J):
-                value = value + end[j, i]
+                value = value + end[j, start + i]
                 csum[j, i] = value * scale
             return carry
 
-        lax.fori_loop(0, width, running, 0)
+        lax.fori_loop(c * width, (c + 1) * width, running, 0)
         sum_copy(c).start()
-    for c in range(chunks):
-        out_copy(c).wait()
-        sum_copy(c).wait()
+    return [sum_copy(c) for c in range(chunks)]
+
+
+def first_out_kernel(scale, chunks, split, end, under, sums_out, field_out, done, csum, sem, field_sem):
+    whole = pltpu.make_async_copy(end, field_out, field_sem)
+    whole.start()
+    second_core = lax.rem(lax.axis_index("pz"), 2) == 1
+
+    def columns(size):
+        for copy in columns_out(scale, chunks, 0, size, end, under, sums_out, csum, sem):
+            copy.wait()
+
+    @pl.when(second_core)
+    def _():
+        columns(split)
+
+    @pl.when(jnp.logical_not(second_core))
+    def _():
+        columns(end.shape[1])
+
+    whole.wait()
+    done[...] = jnp.zeros(done.shape, jnp.float32)
+
+
+def rest_out_kernel(scale, chunks, split, end, under_rest, _, sums_out, csum, sem):
+    @pl.when(lax.rem(lax.axis_index("pz"), 2) == 1)
+    def _():
+        for copy in columns_out(scale, chunks, split, end.shape[1] - split, end, under_rest, sums_out, csum, sem):
+            copy.wait()
 
 
 def local(peers, field_now, earlier, speed_square):
     J, I, K, L = field_now.shape
-    chunks = CHUNKS if I % CHUNKS == 0 else 1
-    out_chunks = OUT_CHUNKS if I % OUT_CHUNKS == 0 else 1
     ny = peers[0]
+    split = I * FIRST[0] // FIRST[1]
     f32 = jnp.float32
     dma = pltpu.SemaphoreType.DMA
     anywhere = pl.BlockSpec(memory_space=pltpu.MemorySpace.HBM)
     shape = jax.ShapeDtypeStruct(field_now.shape, f32)
     slots = max(ny - 1, 1)
     resident = pl.BlockSpec(memory_space=pltpu.VMEM)
-    end, under = pl.pallas_call(
-        functools.partial(march_kernel, peers, chunks),
-        out_shape=(pltpu.VMEM((J, I, K, L), f32), pltpu.VMEM((I, K, L), f32)),
+    end, under, total = pl.pallas_call(
+        functools.partial(march_kernel, peers, split),
+        out_shape=(pltpu.VMEM((J, I, K, L), f32), pltpu.VMEM((I, K, L), f32), pltpu.VMEM((I, K, L), f32)),
         in_specs=[anywhere] * 3,
-        out_specs=(resident, resident),
+        out_specs=(resident,) * 3,
         scratch_shapes=[
             pltpu.VMEM((2, J + 2, I + 2, K, L), f32),
             pltpu.VMEM((J, I, K, L), f32),
-            pltpu.VMEM((I, K, L), f32),
             pltpu.VMEM((slots, I, K, L), f32),
             pltpu.VMEM((STEPS, 2, J, I, L), f32),
             pltpu.VMEM((STEPS, 2, J, I, L), f32),
             dma((5,)),
-            dma((STEPS, 2, chunks)),
-            dma((STEPS, 2, chunks)),
+            dma((STEPS, 2, 2)),
+            dma((STEPS, 2, 2)),
             dma((STEPS, 2, 3)),
             dma((STEPS, 2, 3)),
             dma((STEPS, 2, 3)),
             dma((STEPS, 2, 3)),
-            dma((slots, chunks)),
-            dma((slots, chunks)),
+            dma((slots,)),
+            dma((slots,)),
             pltpu.SemaphoreType.REGULAR((2,)),
             pltpu.SemaphoreType.REGULAR((3,)),
         ],
         compiler_params=pltpu.CompilerParams(
-            collective_id=0, has_side_effects=True, vmem_limit_bytes=55 * 1024 * 1024
+            collective_id=0, has_side_effects=True, vmem_limit_bytes=56 * 1024 * 1024
         ),
         name="march",
     )(field_now, earlier, speed_square)
-    return pl.pallas_call(
-        functools.partial(sums_kernel, 1.0 / (J * ny), out_chunks),
-        out_shape=(shape, shape),
+    scale = 1.0 / (J * ny)
+    small = pltpu.CompilerParams(vmem_limit_bytes=16 * 1024 * 1024)
+
+    chunks = OUT_CHUNKS if I % OUT_CHUNKS == 0 and split % OUT_CHUNKS == 0 else 1
+
+    sums, field_end, done = pl.pallas_call(
+        functools.partial(first_out_kernel, scale, chunks, split),
+        out_shape=(shape, shape, pltpu.VMEM((8, L), f32)),
         in_specs=[resident] * 2,
-        out_specs=(anywhere, anywhere),
-        scratch_shapes=[pltpu.VMEM((J, I, K, L), f32), dma((out_chunks,)), dma((out_chunks,))],
-        compiler_params=pltpu.CompilerParams(vmem_limit_bytes=16 * 1024 * 1024),
-        name="sums",
+        out_specs=(anywhere, anywhere, resident),
+        scratch_shapes=[pltpu.VMEM((J, I, K, L), f32), dma((chunks,)), dma],
+        compiler_params=small,
+        name="first_out",
     )(end, under)
+    rest = I - split
+    under_rest = pl.pallas_call(
+        functools.partial(rest_kernel, ny, split),
+        out_shape=pltpu.VMEM((rest, K, L), f32),
+        in_specs=[resident] * 3,
+        out_specs=resident,
+        scratch_shapes=[pltpu.VMEM((slots, rest, K, L), f32), dma((slots,)), dma((slots,))],
+        compiler_params=pltpu.CompilerParams(
+            collective_id=1, has_side_effects=True, vmem_limit_bytes=16 * 1024 * 1024
+        ),
+        name="rest",
+    )(total, under, done)
+    sums = pl.pallas_call(
+        functools.partial(rest_out_kernel, scale, chunks, split),
+        out_shape=shape,
+        in_specs=[resident] * 2 + [anywhere],
+        out_specs=anywhere,
+        input_output_aliases={2: 0},
+        scratch_shapes=[pltpu.VMEM((J, rest, K, L), f32), dma((chunks,))],
+        compiler_params=small,
+        name="rest_out",
+    )(end, under_rest, sums)
+    return sums, field_end
 
 
 def solution(mesh):

time: 110 us -> 107 us (0.973)
  Pallas kernels: 109 us -> 106 us
    pallas_call x2 -> x4, Pallas kernels: 109 us -> 106 us  [the longest x1 103 us: local(): pl.pallas_call(functools.partial(march_kernel, peers, split), out_shape=(...]
where the time goes in v2:
time: 107 us
  Pallas kernels  106 us (99%)
    pallas_call x1, Pallas kernels, local(): pl.pallas_call(functools.partial(march_kernel, peers, split), out_shape=(...  103 us
    pallas_call x1, Pallas kernels, local(): pl.pallas_call(functools.partial(first_out_kernel, scale, chunks, split),...  3.34 us

profile of v2, /device:TPU:0, one launch (start us, length us, event | category | flops | bytes accessed | tf_op | source)
XLA Modules:
  0.0 106.9 jit_solution(2778775551863431099)
XLA Ops:
  0.6 102.8 %march.1 = (f32[8,16,64,128]{3,2,1,0:T(8,128)S(1)}, f32[16,64,128]{2,1,0:T(8,128)S(1)}, f32[16,64,128]{2,1,0:T(8,128)S(1)}) custom-call(f32[8,16,64,128]{3,2,1,0:T(8,128)} %field.1, f32[8,16,64,128]{3,2,1,0:T(8,128)} %before.1, f32[8,16,64,128]{3,2,1,0:T(8,128)} %speed.1), custom_call_target="tpu_custom_call" | custom-call | tf_op jit(solution)/shard_map/march/pallas_call | solution.py:362
  103.4 3.3 %first_out.1 = (f32[8,16,64,128]{3,2,1,0:T(8,128)}, f32[8,16,64,128]{3,2,1,0:T(8,128)}, f32[8,128]{1,0:T(8,128)S(1)}) custom-call(f32[8,16,64,128]{3,2,1,0:T(8,128)S(1)} %get-tuple-element.8.end, f32[16,64,128]{2,1,0:T(8,128)S(1)} %get-tuple-element.10.under), custom_call_target="tpu_custom_call" | custom-call | tf_op jit(solution)/shard_map/first_out/pallas_call | solution.py:395
  106.8 0.1 rest.1.under_rest
  106.8 0.1 rest_out.1

commit v3 on v2

--- a/solution.py
+++ b/solution.py
@@ -167,7 +167,8 @@
     def total_copy(d, first):
         here = pl.ds(0, split if first else I)
         return remote(
-            total.at[here], below.at[d - 1, here], t_send.at[d - 1], t_recv.at[d - 1], {"py": lax.rem(my + d, ny)}
+            total.at[here], under.at[here] if d == 1 else below.at[d - 2, here], t_send.at[d - 1], t_recv.at[d - 1],
+            {"py": lax.rem(my + d, ny)},
         )
 
     def for_totals(mine, first, act):
@@ -238,11 +239,15 @@
                     if s == order(t)[1]:
                         for_totals(True, c == 0, lambda copy, d: copy.start())
 
-    under[...] = jnp.zeros((I, K, L), jnp.float32)
+    @pl.when(my == 0)
+    def _():
+        under[...] = jnp.zeros((I, K, L), jnp.float32)
+
     for first in (True, False):
         def take(copy, d, size=split if first else I):
             copy.wait_recv()
-            under[:size] = under[:size] + below[d - 1, :size]
+            if d > 1:
+                under[:size] = under[:size] + below[d - 2, :size]
 
         for_totals(False, first, take)
 
@@ -257,7 +262,7 @@
         for_totals(True, first, lambda copy, d: copy.wait_send())
 
 
-def rest_kernel(ny, split, total, under, _, under_rest, below, send, recv):
+def rest_kernel(ny, split, total, _, under_rest, below, send, recv):
     size = total.shape[0] - split
     my = lax.axis_index("py")
     there = pl.ds(split, size)
@@ -265,11 +270,14 @@
 
     def copy(d):
         return pltpu.make_async_remote_copy(
-            src_ref=total.at[there], dst_ref=below.at[d - 1], send_sem=send.at[d - 1], recv_sem=recv.at[d - 1],
+            src_ref=total.at[there], dst_ref=under_rest if d == 1 else below.at[d - 2],
+            send_sem=send.at[d - 1], recv_sem=recv.at[d - 1],
             device_id={"py": lax.rem(my + d, ny)}, device_id_type=MESH,
         )
 
-    under_rest[...] = under[split:]
+    @pl.when(my == 0)
+    def _():
+        under_rest[...] = jnp.zeros(under_rest.shape, jnp.float32)
 
     @pl.when(second_core)
     def _():
@@ -292,7 +300,8 @@
             @pl.when(my >= d)
             def _(d=d):
                 copy(d).wait_recv()
-                under_rest[...] = under_rest[...] + below[d - 1]
+                if d > 1:
+                    under_rest[...] = under_rest[...] + below[d - 2]
 
         for d in range(1, ny):
             @pl.when(my + d < ny)
@@ -300,8 +309,9 @@
                 copy(d).wait_send()
 
 
-def columns_out(scale, chunks, start, size, end, under, sums_out, csum, sem):
+def columns_out(scale, start, size, end, under, sums_out, csum, sem):
     J = end.shape[0]
+    chunks = max(n for n in range(1, OUT_CHUNKS + 1) if size % n == 0)
     width = size // chunks
 
     def sum_copy(c):
@@ -321,13 +331,13 @@
     return [sum_copy(c) for c in range(chunks)]
 
 
-def first_out_kernel(scale, chunks, split, end, under, sums_out, field_out, done, csum, sem, field_sem):
+def first_out_kernel(scale, split, end, under, sums_out, field_out, done, csum, sem, field_sem):
     whole = pltpu.make_async_copy(end, field_out, field_sem)
     whole.start()
     second_core = lax.rem(lax.axis_index("pz"), 2) == 1
 
     def columns(size):
-        for copy in columns_out(scale, chunks, 0, size, end, under, sums_out, csum, sem):
+        for copy in columns_out(scale, 0, size, end, under, sums_out, csum, sem):
             copy.wait()
 
     @pl.when(second_core)
@@ -342,10 +352,10 @@
     done[...] = jnp.zeros(done.shape, jnp.float32)
 
 
-def rest_out_kernel(scale, chunks, split, end, under_rest, _, sums_out, csum, sem):
+def rest_out_kernel(scale, split, end, under_rest, _, sums_out, csum, sem):
     @pl.when(lax.rem(lax.axis_index("pz"), 2) == 1)
     def _():
-        for copy in columns_out(scale, chunks, split, end.shape[1] - split, end, under_rest, sums_out, csum, sem):
+        for copy in columns_out(scale, split, end.shape[1] - split, end, under_rest, sums_out, csum, sem):
             copy.wait()
 
 
@@ -357,7 +367,7 @@
     dma = pltpu.SemaphoreType.DMA
     anywhere = pl.BlockSpec(memory_space=pltpu.MemorySpace.HBM)
     shape = jax.ShapeDtypeStruct(field_now.shape, f32)
-    slots = max(ny - 1, 1)
+    slots, extra = max(ny - 1, 1), max(ny - 2, 1)
     resident = pl.BlockSpec(memory_space=pltpu.VMEM)
     end, under, total = pl.pallas_call(
         functools.partial(march_kernel, peers, split),
@@ -367,7 +377,7 @@
         scratch_shapes=[
             pltpu.VMEM((2, J + 2, I + 2, K, L), f32),
             pltpu.VMEM((J, I, K, L), f32),
-            pltpu.VMEM((slots, I, K, L), f32),
+            pltpu.VMEM((extra, I, K, L), f32),
             pltpu.VMEM((STEPS, 2, J, I, L), f32),
             pltpu.VMEM((STEPS, 2, J, I, L), f32),
             dma((5,)),
@@ -390,14 +400,12 @@
     scale = 1.0 / (J * ny)
     small = pltpu.CompilerParams(vmem_limit_bytes=16 * 1024 * 1024)
 
-    chunks = OUT_CHUNKS if I % OUT_CHUNKS == 0 and split % OUT_CHUNKS == 0 else 1
-
     sums, field_end, done = pl.pallas_call(
-        functools.partial(first_out_kernel, scale, chunks, split),
+        functools.partial(first_out_kernel, scale, split),
         out_shape=(shape, shape, pltpu.VMEM((8, L), f32)),
         in_specs=[resident] * 2,
         out_specs=(anywhere, anywhere, resident),
-        scratch_shapes=[pltpu.VMEM((J, I, K, L), f32), dma((chunks,)), dma],
+        scratch_shapes=[pltpu.VMEM((J, I, K, L), f32), dma((OUT_CHUNKS,)), dma],
         compiler_params=small,
         name="first_out",
     )(end, under)
@@ -405,21 +413,21 @@
     under_rest = pl.pallas_call(
         functools.partial(rest_kernel, ny, split),
         out_shape=pltpu.VMEM((rest, K, L), f32),
-        in_specs=[resident] * 3,
+        in_specs=[resident] * 2,
         out_specs=resident,
-        scratch_shapes=[pltpu.VMEM((slots, rest, K, L), f32), dma((slots,)), dma((slots,))],
+        scratch_shapes=[pltpu.VMEM((extra, rest, K, L), f32), dma((slots,)), dma((slots,))],
         compiler_params=pltpu.CompilerParams(
             collective_id=1, has_side_effects=True, vmem_limit_bytes=16 * 1024 * 1024
         ),
         name="rest",
-    )(total, under, done)
+    )(total, done)
     sums = pl.pallas_call(
-        functools.partial(rest_out_kernel, scale, chunks, split),
+        functools.partial(rest_out_kernel, scale, split),
         out_shape=shape,
         in_specs=[resident] * 2 + [anywhere],
         out_specs=anywhere,
         input_output_aliases={2: 0},
-        scratch_shapes=[pltpu.VMEM((J, rest, K, L), f32), dma((chunks,))],
+        scratch_shapes=[pltpu.VMEM((J, rest, K, L), f32), dma((OUT_CHUNKS,))],
         compiler_params=small,
         name="rest_out",
     )(end, under_rest, sums)

time: 107 us -> 107 us (level)
  no operation moved by 1% of the time
where the time goes in v3:
time: 107 us
  Pallas kernels  106 us (99%)
    pallas_call x1, Pallas kernels, local(): pl.pallas_call(functools.partial(march_kernel, peers, split), out_shape=(...  103 us
    pallas_call x1, Pallas kernels, local(): pl.pallas_call(functools.partial(first_out_kernel, scale, split), out_sha...  3.34 us

profile of v3, /device:TPU:0, one launch (start us, length us, event | category | flops | bytes accessed | tf_op | source)
XLA Modules:
  0.0 106.9 jit_solution(2047691426962554944)
XLA Ops:
  0.6 102.8 %march.1 = (f32[8,16,64,128]{3,2,1,0:T(8,128)S(1)}, f32[16,64,128]{2,1,0:T(8,128)S(1)}, f32[16,64,128]{2,1,0:T(8,128)S(1)}) custom-call(f32[8,16,64,128]{3,2,1,0:T(8,128)} %field.1, f32[8,16,64,128]{3,2,1,0:T(8,128)} %before.1, f32[8,16,64,128]{3,2,1,0:T(8,128)} %speed.1), custom_call_target="tpu_custom_call" | custom-call | tf_op jit(solution)/shard_map/march/pallas_call | solution.py:372
  103.4 3.3 %first_out.1 = (f32[8,16,64,128]{3,2,1,0:T(8,128)}, f32[8,16,64,128]{3,2,1,0:T(8,128)}, f32[8,128]{1,0:T(8,128)S(1)}) custom-call(f32[8,16,64,128]{3,2,1,0:T(8,128)S(1)} %get-tuple-element.8.end, f32[16,64,128]{2,1,0:T(8,128)S(1)} %get-tuple-element.10.under), custom_call_target="tpu_custom_call" | custom-call | tf_op jit(solution)/shard_map/first_out/pallas_call | solution.py:403
  106.8 0.1 rest.1.under_rest
  106.9 0.1 rest_out.1

commit v4 on v3

--- a/solution.py
+++ b/solution.py
@@ -9,7 +9,7 @@
 
 STEPS = 4
 OUT_CHUNKS = 4
-FIRST = (1, 2)
+FIRST = (7, 16)
 MESH = pl.DeviceIdType.MESH
 
 
@@ -25,7 +25,9 @@
     x_side = ({"px": lax.rem(mx + 1, nx)}, {"px": lax.rem(mx + nx - 1, nx)})
     z_side = ({"pz": lax.rem(mz + 1, nz)}, {"pz": lax.rem(mz + nz - 1, nz)})
     parts = ((1, J - 2), (0, 1), (J - 1, 1))
-    halves = ((0, split), (split, I - split))
+    near = I - max(I // 16, 1)
+    cut = ((0, split), (split, near - split), (near, I - near))
+    sent = ((0, split), (0, near), (near, I - near))
     second_core = lax.rem(mz, 2) == 1
 
     loads = [
@@ -92,7 +94,7 @@
         return (0, 1) if t % 2 == 0 else (1, 0)
 
     def cuts(t, side):
-        return halves if t + 1 == STEPS and side == order(t)[1] else ((0, I),)
+        return cut if t + 1 == STEPS and side == order(t)[1] else ((0, I),)
 
     def j_copy(t, side, c):
         row, rim = ((J - 1, 0), (0, J + 1))[side]
@@ -164,18 +166,18 @@
         else:
             end[j, i] = later
 
-    def total_copy(d, first):
-        here = pl.ds(0, split if first else I)
+    def total_copy(d, c):
+        here = pl.ds(*sent[c])
         return remote(
-            total.at[here], under.at[here] if d == 1 else below.at[d - 2, here], t_send.at[d - 1], t_recv.at[d - 1],
+            total.at[here], under.at[here] if d == 1 else below.at[d - 2, here], t_send.at[d - 1, c], t_recv.at[d - 1, c],
             {"py": lax.rem(my + d, ny)},
         )
 
-    def for_totals(mine, first, act):
+    def for_totals(mine, c, act):
         for d in range(1, ny):
-            @pl.when(jnp.logical_and(second_core if first else jnp.logical_not(second_core), my + d < ny if mine else my >= d))
+            @pl.when(jnp.logical_and(second_core if c == 0 else jnp.logical_not(second_core), my + d < ny if mine else my >= d))
             def _(d=d):
-                act(total_copy(d, first), d)
+                act(total_copy(d, c), d)
 
     for t in range(STEPS):
         last = t + 1 == STEPS
@@ -237,19 +239,19 @@
                     j_copy(t, s, c).wait_recv()
                     lax.fori_loop(start, start + size, outer, 0)
                     if s == order(t)[1]:
-                        for_totals(True, c == 0, lambda copy, d: copy.start())
+                        for_totals(True, c, lambda copy, d: copy.start())
 
     @pl.when(my == 0)
     def _():
         under[...] = jnp.zeros((I, K, L), jnp.float32)
 
-    for first in (True, False):
-        def take(copy, d, size=split if first else I):
+    for c, (start, size) in enumerate(sent):
+        def take(copy, d, here=pl.ds(start, size)):
             copy.wait_recv()
             if d > 1:
-                under[:size] = under[:size] + below[d - 2, :size]
-
-        for_totals(False, first, take)
+                under[here] = under[here] + below[d - 2, here]
+
+        for_totals(False, c, take)
 
     for side in (0, 1):
         for c in range(len(cuts(STEPS - 1, side))):
@@ -258,8 +260,8 @@
             i_copy(STEPS - 1, side, part).wait_send()
             for t in range(STEPS):
                 k_copy(t, side, part).wait_send()
-    for first in (True, False):
-        for_totals(True, first, lambda copy, d: copy.wait_send())
+    for c in range(len(sent)):
+        for_totals(True, c, lambda copy, d: copy.wait_send())
 
 
 def rest_kernel(ny, split, total, _, under_rest, below, send, recv):
@@ -311,14 +313,16 @@
 
 def columns_out(scale, start, size, end, under, sums_out, csum, sem):
     J = end.shape[0]
-    chunks = max(n for n in range(1, OUT_CHUNKS + 1) if size % n == 0)
-    width = size // chunks
+    pieces = min(OUT_CHUNKS, size) - 1
+    bounds = [0] + [1 + (size - 1) * n // max(pieces, 1) for n in range(pieces + 1)]
 
     def sum_copy(c):
-        here = pl.ds(c * width, width)
-        return pltpu.make_async_copy(csum.at[:, here], sums_out.at[:, pl.ds(start + c * width, width)], sem.at[c])
-
-    for c in range(chunks):
+        low, width = bounds[c], bounds[c + 1] - bounds[c]
+        return pltpu.make_async_copy(
+            csum.at[:, pl.ds(low, width)], sums_out.at[:, pl.ds(start + low, width)], sem.at[c]
+        )
+
+    for c in range(pieces + 1):
         def running(i, carry):
             value = under[i]
             for j in range(J):
@@ -326,9 +330,9 @@
                 csum[j, i] = value * scale
             return carry
 
-        lax.fori_loop(c * width, (c + 1) * width, running, 0)
+        lax.fori_loop(bounds[c], bounds[c + 1], running, 0)
         sum_copy(c).start()
-    return [sum_copy(c) for c in range(chunks)]
+    return [sum_copy(c) for c in range(pieces + 1)]
 
 
 def first_out_kernel(scale, split, end, under, sums_out, field_out, done, csum, sem, field_sem):
@@ -381,14 +385,14 @@
             pltpu.VMEM((STEPS, 2, J, I, L), f32),
             pltpu.VMEM((STEPS, 2, J, I, L), f32),
             dma((5,)),
-            dma((STEPS, 2, 2)),
-            dma((STEPS, 2, 2)),
-            dma((STEPS, 2, 3)),
-            dma((STEPS, 2, 3)),
-            dma((STEPS, 2, 3)),
-            dma((STEPS, 2, 3)),
-            dma((slots,)),
-            dma((slots,)),
+            dma((STEPS, 2, 3)),
+            dma((STEPS, 2, 3)),
+            dma((STEPS, 2, 3)),
+            dma((STEPS, 2, 3)),
+            dma((STEPS, 2, 3)),
+            dma((STEPS, 2, 3)),
+            dma((slots, 3)),
+            dma((slots, 3)),
             pltpu.SemaphoreType.REGULAR((2,)),
             pltpu.SemaphoreType.REGULAR((3,)),
         ],

time: 107 us -> 107 us (level)
  no operation moved by 1% of the time
where the time goes in v4:
time: 107 us
  Pallas kernels  106 us (99%)
    pallas_call x1, Pallas kernels, local(): pl.pallas_call(functools.partial(march_kernel, peers, split), out_shape=(...  103 us
    pallas_call x1, Pallas kernels, local(): pl.pallas_call(functools.partial(first_out_kernel, scale, split), out_sha...  3.35 us

profile of v4, /device:TPU:0, one launch (start us, length us, event | category | flops | bytes accessed | tf_op | source)
XLA Modules:
  0.0 106.7 jit_solution(12327984249278983027)
XLA Ops:
  0.6 102.6 %march.1 = (f32[8,16,64,128]{3,2,1,0:T(8,128)S(1)}, f32[16,64,128]{2,1,0:T(8,128)S(1)}, f32[16,64,128]{2,1,0:T(8,128)S(1)}) custom-call(f32[8,16,64,128]{3,2,1,0:T(8,128)} %field.1, f32[8,16,64,128]{3,2,1,0:T(8,128)} %before.1, f32[8,16,64,128]{3,2,1,0:T(8,128)} %speed.1), custom_call_target="tpu_custom_call" | custom-call | tf_op jit(solution)/shard_map/march/pallas_call | solution.py:376
  103.2 3.4 %first_out.1 = (f32[8,16,64,128]{3,2,1,0:T(8,128)}, f32[8,16,64,128]{3,2,1,0:T(8,128)}, f32[8,128]{1,0:T(8,128)S(1)}) custom-call(f32[8,16,64,128]{3,2,1,0:T(8,128)S(1)} %get-tuple-element.8.end, f32[16,64,128]{2,1,0:T(8,128)S(1)} %get-tuple-element.10.under), custom_call_target="tpu_custom_call" | custom-call | tf_op jit(solution)/shard_map/first_out/pallas_call | solution.py:407
  106.6 0.1 rest.1.under_rest
  106.7 0.1 rest_out.1

commit v5 on v2

--- a/solution.py
+++ b/solution.py
@@ -324,17 +324,17 @@
 def first_out_kernel(scale, chunks, split, end, under, sums_out, field_out, done, csum, sem, field_sem):
     whole = pltpu.make_async_copy(end, field_out, field_sem)
     whole.start()
-    second_core = lax.rem(lax.axis_index("pz"), 2) == 1
+    partly = jnp.logical_and(lax.rem(lax.axis_index("pz"), 2) == 1, lax.axis_index("py") > 0)
 
     def columns(size):
         for copy in columns_out(scale, chunks, 0, size, end, under, sums_out, csum, sem):
             copy.wait()
 
-    @pl.when(second_core)
+    @pl.when(partly)
     def _():
         columns(split)
 
-    @pl.when(jnp.logical_not(second_core))
+    @pl.when(jnp.logical_not(partly))
     def _():
         columns(end.shape[1])
 
@@ -343,7 +343,7 @@
 
 
 def rest_out_kernel(scale, chunks, split, end, under_rest, _, sums_out, csum, sem):
-    @pl.when(lax.rem(lax.axis_index("pz"), 2) == 1)
+    @pl.when(jnp.logical_and(lax.rem(lax.axis_index("pz"), 2) == 1, lax.axis_index("py") > 0))
     def _():
         for copy in columns_out(scale, chunks, split, end.shape[1] - split, end, under_rest, sums_out, csum, sem):
             copy.wait()

time: 107 us -> 107 us (level)
  no operation moved by 1% of the time
where the time goes in v5:
time: 107 us
  Pallas kernels  106 us (99%)
    pallas_call x1, Pallas kernels, local(): pl.pallas_call(functools.partial(march_kernel, peers, split), out_shape=(...  103 us
    pallas_call x1, Pallas kernels, local(): pl.pallas_call(functools.partial(first_out_kernel, scale, chunks, split),...  3.34 us

profile of v5, /device:TPU:0, one launch (start us, length us, event | category | flops | bytes accessed | tf_op | source)
XLA Modules:
  0.0 106.9 jit_solution(1979445112312061610)
XLA Ops:
  0.6 102.8 %march.1 = (f32[8,16,64,128]{3,2,1,0:T(8,128)S(1)}, f32[16,64,128]{2,1,0:T(8,128)S(1)}, f32[16,64,128]{2,1,0:T(8,128)S(1)}) custom-call(f32[8,16,64,128]{3,2,1,0:T(8,128)} %field.1, f32[8,16,64,128]{3,2,1,0:T(8,128)} %before.1, f32[8,16,64,128]{3,2,1,0:T(8,128)} %speed.1), custom_call_target="tpu_custom_call" | custom-call | tf_op jit(solution)/shard_map/march/pallas_call | solution.py:362
  103.4 3.3 %first_out.1 = (f32[8,16,64,128]{3,2,1,0:T(8,128)}, f32[8,16,64,128]{3,2,1,0:T(8,128)}, f32[8,128]{1,0:T(8,128)S(1)}) custom-call(f32[8,16,64,128]{3,2,1,0:T(8,128)S(1)} %get-tuple-element.8.end, f32[16,64,128]{2,1,0:T(8,128)S(1)} %get-tuple-element.10.under), custom_call_target="tpu_custom_call" | custom-call | tf_op jit(solution)/shard_map/first_out/pallas_call | solution.py:395
  106.8 0.1 rest.1.under_rest
  106.8 0.1 rest_out.1

commit v6 on v4

--- a/solution.py
+++ b/solution.py
@@ -338,17 +338,17 @@
 def first_out_kernel(scale, split, end, under, sums_out, field_out, done, csum, sem, field_sem):
     whole = pltpu.make_async_copy(end, field_out, field_sem)
     whole.start()
-    second_core = lax.rem(lax.axis_index("pz"), 2) == 1
+    partly = jnp.logical_and(lax.rem(lax.axis_index("pz"), 2) == 1, lax.axis_index("py") > 0)
 
     def columns(size):
         for copy in columns_out(scale, 0, size, end, under, sums_out, csum, sem):
             copy.wait()
 
-    @pl.when(second_core)
+    @pl.when(partly)
     def _():
         columns(split)
 
-    @pl.when(jnp.logical_not(second_core))
+    @pl.when(jnp.logical_not(partly))
     def _():
         columns(end.shape[1])
 
@@ -357,7 +357,7 @@
 
 
 def rest_out_kernel(scale, split, end, under_rest, _, sums_out, csum, sem):
-    @pl.when(lax.rem(lax.axis_index("pz"), 2) == 1)
+    @pl.when(jnp.logical_and(lax.rem(lax.axis_index("pz"), 2) == 1, lax.axis_index("py") > 0))
     def _():
         for copy in columns_out(scale, split, end.shape[1] - split, end, under_rest, sums_out, csum, sem):
             copy.wait()

time: 107 us -> 107 us (level)
  no operation moved by 1% of the time
where the time goes in v6:
time: 107 us
  Pallas kernels  106 us (99%)
    pallas_call x1, Pallas kernels, local(): pl.pallas_call(functools.partial(march_kernel, peers, split), out_shape=(...  103 us
    pallas_call x1, Pallas kernels, local(): pl.pallas_call(functools.partial(first_out_kernel, scale, split), out_sha...  3.35 us

profile of v6, /device:TPU:0, one launch (start us, length us, event | category | flops | bytes accessed | tf_op | source)
XLA Modules:
  0.0 106.7 jit_solution(6694450326656421202)
XLA Ops:
  0.6 102.6 %march.1 = (f32[8,16,64,128]{3,2,1,0:T(8,128)S(1)}, f32[16,64,128]{2,1,0:T(8,128)S(1)}, f32[16,64,128]{2,1,0:T(8,128)S(1)}) custom-call(f32[8,16,64,128]{3,2,1,0:T(8,128)} %field.1, f32[8,16,64,128]{3,2,1,0:T(8,128)} %before.1, f32[8,16,64,128]{3,2,1,0:T(8,128)} %speed.1), custom_call_target="tpu_custom_call" | custom-call | tf_op jit(solution)/shard_map/march/pallas_call | solution.py:376
  103.2 3.4 %first_out.1 = (f32[8,16,64,128]{3,2,1,0:T(8,128)}, f32[8,16,64,128]{3,2,1,0:T(8,128)}, f32[8,128]{1,0:T(8,128)S(1)}) custom-call(f32[8,16,64,128]{3,2,1,0:T(8,128)S(1)} %get-tuple-element.8.end, f32[16,64,128]{2,1,0:T(8,128)S(1)} %get-tuple-element.10.under), custom_call_target="tpu_custom_call" | custom-call | tf_op jit(solution)/shard_map/first_out/pallas_call | solution.py:407
  106.6 0.1 rest.1.under_rest
  106.7 0.1 rest_out.1

commit v7 on v6

--- a/solution.py
+++ b/solution.py
@@ -9,7 +9,7 @@
 
 STEPS = 4
 OUT_CHUNKS = 4
-FIRST = (7, 16)
+FIRST = (3, 8)
 MESH = pl.DeviceIdType.MESH
 
 

time: 107 us -> 107 us (level)
  no operation moved by 1% of the time
where the time goes in v7:
time: 107 us
  Pallas kernels  106 us (99%)
    pallas_call x1, Pallas kernels, local(): pl.pallas_call(functools.partial(march_kernel, peers, split), out_shape=(...  103 us
    pallas_call x1, Pallas kernels, local(): pl.pallas_call(functools.partial(first_out_kernel, scale, split), out_sha...  3.35 us

profile of v7, /device:TPU:0, one launch (start us, length us, event | category | flops | bytes accessed | tf_op | source)
XLA Modules:
  0.0 106.8 jit_solution(9913751010099811925)
XLA Ops:
  0.6 102.6 %march.1 = (f32[8,16,64,128]{3,2,1,0:T(8,128)S(1)}, f32[16,64,128]{2,1,0:T(8,128)S(1)}, f32[16,64,128]{2,1,0:T(8,128)S(1)}) custom-call(f32[8,16,64,128]{3,2,1,0:T(8,128)} %field.1, f32[8,16,64,128]{3,2,1,0:T(8,128)} %before.1, f32[8,16,64,128]{3,2,1,0:T(8,128)} %speed.1), custom_call_target="tpu_custom_call" | custom-call | tf_op jit(solution)/shard_map/march/pallas_call | solution.py:376
  103.3 3.4 %first_out.1 = (f32[8,16,64,128]{3,2,1,0:T(8,128)}, f32[8,16,64,128]{3,2,1,0:T(8,128)}, f32[8,128]{1,0:T(8,128)S(1)}) custom-call(f32[8,16,64,128]{3,2,1,0:T(8,128)S(1)} %get-tuple-element.8.end, f32[16,64,128]{2,1,0:T(8,128)S(1)} %get-tuple-element.10.under), custom_call_target="tpu_custom_call" | custom-call | tf_op jit(solution)/shard_map/first_out/pallas_call | solution.py:407
  106.6 0.1 rest.1.under_rest
  106.7 0.1 rest_out.1
